TPU v7x, 32 devices: a whole 2x2x4 slice. The times are simulated.
32 devices in a mesh: dp: 8 (over y, x, core), tensor: 4 (over z).
Axes of the slice: x: 2, y: 2, z: 4, core: 2. Of those that a mesh axis runs over, the one named last changes fastest.
Arguments:
- block_input: bfloat16 [8192, 2048], P('dp'), may hold values from -24 to 24
- segments: int32 [8192], P('dp'), may hold values from 0 to 15, never falling along the last dimension, each value on 1 to 2048 neighbouring positions
- norm_gain: bfloat16 [2048], P('dp'), may hold values from 0.5 to 1.5
- norm_bias: bfloat16 [2048], P('dp'), may hold values from -1.75 to 1.75
- qkv_weight: bfloat16 [2048, 3, 2048], P('dp', None, 'tensor'), may hold values from -1 to 1
- query_value_bias: bfloat16 [2, 32, 64], P(None, 'tensor', 'dp'), may hold values from -1.75 to 1.75
- key_bias: bfloat16 [32, 32], P('tensor', 'dp'), may hold values from -3 to 3
- dense_weight: bfloat16 [2048, 2048], P('tensor', 'dp'), may hold values from -1.5 to 1.5
- dense_bias: bfloat16 [2048], P('dp'), may hold values from -1.75 to 1.75
- up_weight: bfloat16 [2048, 8192], P('dp', 'tensor'), may hold values from -0.125 to 0.125
- up_bias: bfloat16 [128, 64], P('tensor', 'dp'), may hold values from -1.75 to 1.75
- down_weight: bfloat16 [8192, 2048], P('tensor', 'dp'), may hold values from -0.0625 to 0.0625
- down_bias: bfloat16 [2048], P('dp'), may hold values from -1.75 to 1.75
- cotangent: bfloat16 [8192, 2048], P('dp'), may hold values from -8 to 8
Outputs:
- block_output: bfloat16 [8192, 2048], P('dp')
- input_grad: float32 [8192, 2048], P('dp')
- norm_gain_grad: float32 [2048], P('dp')
- norm_bias_grad: float32 [2048], P('dp')
- qkv_weight_grad: float32 [2048, 3, 2048], P('dp', None, 'tensor')
- query_value_bias_grad: float32 [2, 32, 64], P(None, 'tensor', 'dp')
- key_bias_grad: float32 [32, 32], P('tensor', 'dp')
- dense_weight_grad: float32 [2048, 2048], P('tensor', 'dp')
- dense_bias_grad: float32 [2048], P('dp')
- up_weight_grad: float32 [2048, 8192], P('dp', 'tensor')
- up_bias_grad: float32 [128, 64], P('tensor', 'dp')
- down_weight_grad: float32 [8192, 2048], P('tensor', 'dp')
- down_bias_grad: float32 [2048], P('dp')
Inputs may be any that keep to these rules, and one draw needn't show every extreme that they name: `segments`: segment numbers never fall along the tokens; each segment has 1 to 2048 tokens, one exactly 2048.
All inputs are finite; a program needn't handle non-finite values.
Results may differ from a plain program's by a relative error of at most 0.015.
The roundings to bfloat16 on the way count: a program that leaves them out, or rounds other values in their place, can miss the bound.
Values may be sent and summed in bfloat16 or wider, within the bound.
A program may use at most 256 MiB of HBM per device.

v0:
```python
import math
import jax
import jax.numpy as jnp
from jax import lax
from jax.sharding import PartitionSpec as P

HEAD = 64
ROT = 32
SEQ = 512
EPSILON = 1e-05
SCALE = 0.125
NEGATIVE = -1e30


def rotary_tables(seg_rows):
    seq_len = seg_rows.shape[1]
    position = jnp.arange(seq_len, dtype=jnp.int32)
    starting = jnp.concatenate(
        [jnp.ones((seg_rows.shape[0], 1), dtype=jnp.bool_), seg_rows[:, 1:] != seg_rows[:, :-1]],
        axis=1,
    )
    starts = lax.cummax(jnp.where(starting, position[None, :], jnp.int32(0)), axis=1)
    offset = (position[None, :] - starts).astype(jnp.float32)
    halfway = ROT // 2
    inverse = 10000.0 ** (-(jnp.arange(halfway, dtype=jnp.float32) * (2.0 / ROT)))
    angles = offset[:, :, None] * inverse
    return (jnp.cos(angles), jnp.sin(angles))


def rotate(tensor, cosine_table, sine_table, direction):
    halfway = ROT // 2
    leading = tensor[..., :halfway]
    trailing = tensor[..., halfway:ROT]
    others = tensor[..., ROT:]
    cosine_part = cosine_table[:, :, None, :]
    sine_part = sine_table[:, :, None, :] * direction
    return jnp.concatenate(
        [
            leading * cosine_part - trailing * sine_part,
            trailing * cosine_part + leading * sine_part,
            others,
        ],
        axis=-1,
    )


def allowed_pairs(seg_rows):
    seq_len = seg_rows.shape[1]
    position = jnp.arange(seq_len, dtype=jnp.int32)
    causal = position[:, None] >= position[None, :]
    same_doc = seg_rows[:, :, None] == seg_rows[:, None, :]
    return (same_doc & causal[None])[:, None]


def gelu_tanh(inputs):
    return jax.nn.gelu(inputs, approximate=True)


def masked_scores(queries, key_rows, allowed):
    scores = (
        jnp.einsum("nqhd,nkhd->nhqk", queries, key_rows, preferred_element_type=jnp.float32) * SCALE
    )
    return jnp.where(allowed, scores, NEGATIVE)


def attend_group(placeholder, inputs):
    queries, key_rows, values, allowed = inputs
    scores = masked_scores(queries, key_rows, allowed)
    row_max = jnp.max(scores, axis=-1, keepdims=True)
    row_total = jnp.sum(jnp.exp(scores - row_max), axis=-1, keepdims=True)
    log_total = row_max + jnp.log(row_total)
    prob_low = jnp.exp(scores - log_total).astype(jnp.bfloat16)
    mixed_part = jnp.einsum(
        "nhqk,nkhd->nqhd", prob_low, values, preferred_element_type=jnp.float32
    ).astype(jnp.bfloat16)
    return (placeholder, (mixed_part, log_total))


def attend_back_group(placeholder, inputs):
    queries, key_rows, values, allowed, log_total, grad_mixed = inputs
    scores = masked_scores(queries, key_rows, allowed)
    probabilities = jnp.exp(scores - log_total)
    prob_low = probabilities.astype(jnp.bfloat16)
    grad_values = jnp.einsum(
        "nhqk,nqhd->nkhd", prob_low, grad_mixed, preferred_element_type=jnp.float32
    )
    grad_probs = jnp.einsum(
        "nqhd,nkhd->nhqk", grad_mixed, values, preferred_element_type=jnp.float32
    )
    row_delta = jnp.sum(probabilities * grad_probs, axis=-1, keepdims=True)
    grad_scores = (probabilities * (grad_probs - row_delta) * SCALE).astype(jnp.bfloat16)
    grad_queries = jnp.einsum(
        "nhqk,nkhd->nqhd", grad_scores, key_rows, preferred_element_type=jnp.float32
    )
    grad_keys = jnp.einsum(
        "nhqk,nqhd->nkhd", grad_scores, queries, preferred_element_type=jnp.float32
    )
    return (placeholder, (grad_queries, grad_keys, grad_values))


def local(
    block_input,
    segments,
    norm_gain,
    norm_bias,
    qkv_weight,
    query_value_bias,
    key_bias,
    dense_weight,
    dense_bias,
    up_weight,
    up_bias,
    down_weight,
    down_bias,
    cotangent,
):
    gathered = (
        lax.all_gather(norm_gain, "dp", axis=0, tiled=True),
        lax.all_gather(norm_bias, "dp", axis=0, tiled=True),
        lax.all_gather(qkv_weight, "dp", axis=0, tiled=True),
        lax.all_gather(query_value_bias, "dp", axis=2, tiled=True),
        lax.all_gather(key_bias, "dp", axis=1, tiled=True),
        lax.all_gather(dense_weight, "dp", axis=1, tiled=True),
        lax.all_gather(dense_bias, "dp", axis=0, tiled=True),
        lax.all_gather(up_weight, "dp", axis=0, tiled=True),
        lax.all_gather(up_bias, "dp", axis=1, tiled=True),
        lax.all_gather(down_weight, "dp", axis=1, tiled=True),
        lax.all_gather(down_bias, "dp", axis=0, tiled=True),
    )
    (
        gain_all,
        shift_all,
        qkv_all,
        qv_all,
        key_all,
        dense_all,
        dense_shift_all,
        up_all,
        up_shift_all,
        down_all,
        down_shift_all,
    ) = gathered
    row_count, model_width = block_input.shape
    local_width = qkv_all.shape[2]
    heads_here = local_width // HEAD
    seqs_here = row_count // SEQ
    per_step = math.gcd(seqs_here, max(1, 512 // SEQ))
    groups = seqs_here // per_step

    def to_groups(tensor):
        return tensor.reshape((groups, per_step) + tensor.shape[1:])

    def from_groups(tensor):
        return tensor.reshape((seqs_here,) + tensor.shape[2:])

    widened = block_input.astype(jnp.float32)
    row_mean = jnp.mean(widened, axis=1, keepdims=True)
    centred = widened - row_mean
    row_var = jnp.mean(centred * centred, axis=1, keepdims=True)
    inv_std = lax.rsqrt(row_var + EPSILON)
    normed = centred * inv_std
    normed_low = (normed * gain_all.astype(jnp.float32) + shift_all.astype(jnp.float32)).astype(
        jnp.bfloat16
    )
    qkv_flat = qkv_all.reshape(model_width, 3 * local_width)
    projected = jnp.dot(normed_low, qkv_flat, preferred_element_type=jnp.float32).reshape(
        seqs_here, SEQ, 3, heads_here, HEAD
    )
    seq_segs = segments.reshape(seqs_here, SEQ)
    cosine_table, sine_table = rotary_tables(seq_segs)
    allowed = allowed_pairs(seq_segs)
    qv_wide = qv_all.astype(jnp.float32)
    key_full = jnp.concatenate(
        [key_all.astype(jnp.float32), jnp.zeros((heads_here, HEAD - ROT), jnp.float32)], axis=1
    )
    queries = rotate(projected[:, :, 0] + qv_wide[0], cosine_table, sine_table, 1.0).astype(
        jnp.bfloat16
    )
    key_rows = rotate(projected[:, :, 1] + key_full, cosine_table, sine_table, 1.0).astype(
        jnp.bfloat16
    )
    values = (projected[:, :, 2] + qv_wide[1]).astype(jnp.bfloat16)
    placeholder = jnp.zeros((), jnp.float32)
    group_inputs = (to_groups(queries), to_groups(key_rows), to_groups(values), to_groups(allowed))
    unused, (mixed_groups, log_groups) = lax.scan(attend_group, placeholder, group_inputs)
    mixed_rows = mixed_groups.reshape(row_count, local_width)
    hidden = jnp.dot(normed_low, up_all, preferred_element_type=jnp.float32) + up_shift_all.reshape(
        -1
    ).astype(jnp.float32)
    activated = gelu_tanh(hidden).astype(jnp.bfloat16)
    branches = jnp.dot(mixed_rows, dense_all, preferred_element_type=jnp.float32) + jnp.dot(
        activated, down_all, preferred_element_type=jnp.float32
    )
    dense_shift = dense_shift_all.astype(jnp.float32)
    down_shift = down_shift_all.astype(jnp.float32)
    summed_out = lax.psum(branches, "tensor")
    block_output = (widened + summed_out + dense_shift + down_shift).astype(jnp.bfloat16)
    gain_back, qkv_back, dense_back, up_back, down_back = (
        lax.all_gather(norm_gain, "dp", axis=0, tiled=True),
        lax.all_gather(qkv_weight, "dp", axis=0, tiled=True),
        lax.all_gather(dense_weight, "dp", axis=1, tiled=True),
        lax.all_gather(up_weight, "dp", axis=0, tiled=True),
        lax.all_gather(down_weight, "dp", axis=1, tiled=True),
    )
    grad_wide = cotangent.astype(jnp.float32)
    grad_bias_out = jnp.sum(grad_wide, axis=0)
    grad_dense = jnp.dot(mixed_rows.T, cotangent, preferred_element_type=jnp.float32)
    grad_down = jnp.dot(activated.T, cotangent, preferred_element_type=jnp.float32)
    grad_mixed = (
        jnp.dot(cotangent, dense_back.T, preferred_element_type=jnp.float32)
        .astype(jnp.bfloat16)
        .reshape(seqs_here, SEQ, heads_here, HEAD)
    )
    grad_act = jnp.dot(cotangent, down_back.T, preferred_element_type=jnp.float32)
    grad_hidden = jax.vjp(gelu_tanh, hidden)[1](grad_act)[0]
    grad_up_bias = jnp.sum(grad_hidden, axis=0).reshape(up_shift_all.shape)
    grad_hidden_low = grad_hidden.astype(jnp.bfloat16)
    grad_up = jnp.dot(normed_low.T, grad_hidden_low, preferred_element_type=jnp.float32)
    back_inputs = group_inputs + (log_groups, to_groups(grad_mixed))
    unused_back, (query_groups, key_groups, value_groups) = lax.scan(
        attend_back_group, placeholder, back_inputs
    )
    grad_queries = rotate(from_groups(query_groups), cosine_table, sine_table, -1.0)
    grad_keys = rotate(from_groups(key_groups), cosine_table, sine_table, -1.0)
    grad_values = from_groups(value_groups)
    grad_qv = jnp.stack([jnp.sum(grad_queries, axis=(0, 1)), jnp.sum(grad_values, axis=(0, 1))])
    grad_key_bias = jnp.sum(grad_keys[..., :ROT], axis=(0, 1))
    grad_projected = (
        jnp.stack([grad_queries, grad_keys, grad_values], axis=2)
        .reshape(row_count, 3 * local_width)
        .astype(jnp.bfloat16)
    )
    grad_qkv = jnp.dot(normed_low.T, grad_projected, preferred_element_type=jnp.float32).reshape(
        model_width, 3, local_width
    )
    grad_normed_part = jnp.dot(
        grad_projected,
        qkv_back.reshape(model_width, 3 * local_width).T,
        preferred_element_type=jnp.float32,
    ) + jnp.dot(grad_hidden_low, up_back.T, preferred_element_type=jnp.float32)
    grad_normed = lax.psum(grad_normed_part.astype(jnp.bfloat16), "tensor").astype(jnp.float32)
    grad_gain = jnp.sum(grad_normed * normed, axis=0)
    grad_shift = jnp.sum(grad_normed, axis=0)
    scaled = grad_normed * gain_back.astype(jnp.float32)
    input_grad = (
        inv_std
        * (
            scaled
            - jnp.mean(scaled, axis=1, keepdims=True)
            - normed * jnp.mean(scaled * normed, axis=1, keepdims=True)
        )
        + grad_wide
    )
    summed = (
        lax.psum_scatter(grad_gain, "dp", scatter_dimension=0, tiled=True),
        lax.psum_scatter(grad_shift, "dp", scatter_dimension=0, tiled=True),
        lax.psum_scatter(grad_qkv, "dp", scatter_dimension=0, tiled=True),
        lax.psum_scatter(grad_qv, "dp", scatter_dimension=2, tiled=True),
        lax.psum_scatter(grad_key_bias, "dp", scatter_dimension=1, tiled=True),
        lax.psum_scatter(grad_dense, "dp", scatter_dimension=1, tiled=True),
        lax.psum_scatter(grad_bias_out, "dp", scatter_dimension=0, tiled=True),
        lax.psum_scatter(grad_up, "dp", scatter_dimension=0, tiled=True),
        lax.psum_scatter(grad_up_bias, "dp", scatter_dimension=1, tiled=True),
        lax.psum_scatter(grad_down, "dp", scatter_dimension=1, tiled=True),
    )
    return (
        block_output,
        input_grad,
        summed[0],
        summed[1],
        summed[2],
        summed[3],
        summed[4],
        summed[5],
        summed[6],
        summed[7],
        summed[8],
        summed[9],
        summed[6],
    )


def solution(mesh):
    in_specs = (
        P("dp", None),
        P("dp"),
        P("dp"),
        P("dp"),
        P("dp", None, "tensor"),
        P(None, "tensor", "dp"),
        P("tensor", "dp"),
        P("tensor", "dp"),
        P("dp"),
        P("dp", "tensor"),
        P("tensor", "dp"),
        P("tensor", "dp"),
        P("dp"),
        P("dp", None),
    )
    out_specs = (
        P("dp", None),
        P("dp", None),
        P("dp"),
        P("dp"),
        P("dp", None, "tensor"),
        P(None, "tensor", "dp"),
        P("tensor", "dp"),
        P("tensor", "dp"),
        P("dp"),
        P("dp", "tensor"),
        P("tensor", "dp"),
        P("tensor", "dp"),
        P("dp"),
    )
    return jax.shard_map(local, mesh=mesh, in_specs=in_specs, out_specs=out_specs, check_vma=False)
```

profile of v0, /device:TPU:0, one launch (start us, length us, event | category | flops | bytes accessed | tf_op | source)
XLA Modules:
  0.0 1116.1 jit_solution(14657728340286387230)
XLA Ops:
  22.3 10.4 all-gather.1
  32.7 9.1 all-gather
  41.8 8.0 all-gather.2
  49.8 9.2 all_gather.45
  59.8 8.6 all_gather.41
  74.7 6.2 convolution_convert_fusion
  89.3 10.1 fusion.146
  101.6 13.5 %while.26 = (s32[]{:T(128)}, bf16[2,1,512,8,64]{2,4,3,1,0:T(8,128)(2,1)}, f32[2,1,8,512,1]{3,2,4,1,0:T(8,128)S(1)}, bf16[2,1,512,8,64]{2,4,3,1,0:T(8,128)(2,1)},...) while((s32[]{:T(128)}, ...), condition=%wide.region_7.8_spmd, body=%wide.region_4.7_spmd.sunk | while | flops 560197632 | bytes 41289912 | solution.py:185
  115.0 85.6 %while.27 = (s32[]{:T(128)}, f32[2,1,512,8,64]{2,4,3,1,0:T(8,128)}, f32[2,1,512,8,64]{2,4,3,1,0:T(8,128)}, f32[2,1,512,8,64]{2,4,3,1,0:T(8,128)}, bf16[2,1,512,8...) while((s32[]{:T(128)}, f32[2,1,512,8,64]{2,4,3,1,0:T(8,128)}, ...), condition=%wide.region_11.12_spmd, body=%wide.region_9.11_spmd.sunk | while | flops 1396712448 | bytes 159765776 | solution.py:220
  128.5 14.5 %fusion.204 = f32[2,1,512,8,64]{2,4,3,1,0:T(8,128)} fusion(f32[2,1,512,8,64]{2,4,3,1,0:T(8,128)} %get-tuple-element.472, s32[]{:T(128)S(6)} %copy.169, f32[8,512,512]{1,2,0:T(8,128)} %fusion.201, f32[8,512,512]{1,2,0:T(8,128)} %copy-done, f32[8,512]{1,0:T(8,128)S(1)} %dynamic-slice_bitcast_fusion.7, ...), kind=kOutput, calls=%fused_computation.46.clone.1 | convolution fusion | flops 291508736 | bytes 35685376 | tf_op jit(solution)/shard_map/while/body/eval_jaxpr/nhqk,nqhd->nkhd/dot_general | solution.py:95
  143.0 14.4 %fusion.203 = f32[2,1,512,8,64]{2,4,3,1,0:T(8,128)} fusion(f32[2,1,512,8,64]{2,4,3,1,0:T(8,128)} %get-tuple-element.471, s32[]{:T(128)S(6)} %copy.169, f32[8,512,512]{1,2,0:T(8,128)} %fusion.201, f32[8,512,512]{1,2,0:T(8,128)} %copy-done, f32[8,512]{1,0:T(8,128)S(1)} %dynamic-slice_bitcast_fusion.7, ...), kind=kOutput, calls=%fused_computation.44.clone.1 | convolution fusion | flops 291508736 | bytes 35685376 | tf_op jit(solution)/shard_map/while/body/eval_jaxpr/nhqk,nkhd->nqhd/dot_general | solution.py:92
  170.4 15.7 %fusion.204 = f32[2,1,512,8,64]{2,4,3,1,0:T(8,128)} fusion(f32[2,1,512,8,64]{2,4,3,1,0:T(8,128)} %get-tuple-element.472, s32[]{:T(128)S(6)} %copy.169, f32[8,512,512]{1,2,0:T(8,128)} %fusion.201, f32[8,512,512]{1,2,0:T(8,128)} %copy-done, f32[8,512]{1,0:T(8,128)S(1)} %dynamic-slice_bitcast_fusion.7, ...), kind=kOutput, calls=%fused_computation.46.clone.1 | convolution fusion | flops 291508736 | bytes 35685376 | tf_op jit(solution)/shard_map/while/body/eval_jaxpr/nhqk,nqhd->nkhd/dot_general | solution.py:95
  186.0 14.4 %fusion.203 = f32[2,1,512,8,64]{2,4,3,1,0:T(8,128)} fusion(f32[2,1,512,8,64]{2,4,3,1,0:T(8,128)} %get-tuple-element.471, s32[]{:T(128)S(6)} %copy.169, f32[8,512,512]{1,2,0:T(8,128)} %fusion.201, f32[8,512,512]{1,2,0:T(8,128)} %copy-done, f32[8,512]{1,0:T(8,128)S(1)} %dynamic-slice_bitcast_fusion.7, ...), kind=kOutput, calls=%fused_computation.44.clone.1 | convolution fusion | flops 291508736 | bytes 35685376 | tf_op jit(solution)/shard_map/while/body/eval_jaxpr/nhqk,nkhd->nqhd/dot_general | solution.py:92
  211.5 15.6 %fusion.147 = f32[1024,2048]{1,0:T(8,128)} fusion(bf16[1024,2048]{1,0:T(8,128)(2,1)} %fusion.106, bf16[2048,2048]{1,0:T(8,128)(2,1)} %all-gather.14.cloned.1.call-done), kind=kOutput, calls=%fused_computation.179 | convolution fusion | flops 8589934592 | bytes 20971520 | tf_op jit(solution)/shard_map/dot_general | solution.py:187
  227.1 19.2 %fusion.143 = (f32[2048]{0:T(1024)S(1)}, bf16[1024,2048]{1,0:T(8,128)(2,1)S(1)}) fusion(f32[1024,2048]{1,0:T(8,128)} %fusion.147, f32[2048]{0:T(1024)S(1)} %copy-done.25, bf16[1024,2048]{1,0:T(8,128)(2,1)} %param.31, bf16[2048,2048]{1,0:T(8,128)(2,1)} %all-gather.16.cloned.1.call-done), kind=kOutput, calls=%fused_computation.176 | convolution fusion | flops 8636069888 | bytes 25182208 | tf_op jit(solution)/shard_map/dot_general | solution.py:214
  246.4 11.1 fusion.129
  257.4 12.7 %add_convert_fusion = bf16[1024,2048]{1,0:T(8,128)(2,1)} fusion(f32[1024,2048]{1,0:T(8,128)} %fusion.129, bf16[1024,1536]{0,1:T(8,128)(2,1)S(1)} %bitcast.234, bf16[2048,1536]{0,1:T(8,128)(2,1)} %bitcast.255), kind=kOutput, calls=%fused_computation.111 | convolution fusion | flops 6446645248 | bytes 22020096 | tf_op jit(solution)/shard_map/dot_general | solution.py:236
  272.7 16.4 %fusion.142 = f32[1024,2048]{1,0:T(8,128)S(1)} fusion(bf16[2048,2048]{1,0:T(8,128)(2,1)} %all-gather.16.cloned.1.call-done, f32[1024,2048]{1,0:T(8,128)} %fusion.147, f32[2048]{0:T(1024)S(1)} %copy-done.25), kind=kOutput, calls=%fused_computation.175 | convolution fusion | flops 8610906112 | bytes 25174016 | tf_op jit(solution)/shard_map/dot_general | solution.py:191
  295.0 6.5 fusion.148
  301.6 12.7 %fusion.121 = f32[2048,3,512]{2,0,1:T(8,128)} fusion(bf16[3,512,1024]{2,1,0:T(8,128)(2,1)} %bitcast.235, bf16[1024,2048]{1,0:T(8,128)(2,1)} %fusion.106), kind=kOutput, calls=%fused_computation.114 | convolution fusion | flops 6442450944 | bytes 19922944 | tf_op jit(solution)/shard_map/dot_general | solution.py:233
  314.3 17.3 %fusion.141 = f32[2048,2048]{1,0:T(8,128)} fusion(bf16[1024,2048]{1,0:T(8,128)(2,1)} %param.31, f32[1024,2048]{1,0:T(8,128)} %fusion.147, f32[2048]{0:T(1024)S(1)} %copy-done.25), kind=kOutput, calls=%fused_computation.174 | convolution fusion | flops 8610906112 | bytes 29368320 | tf_op jit(solution)/shard_map/dot_general | solution.py:208
  331.9 15.2 %fusion.127 = f32[2048,2048]{1,0:T(8,128)} fusion(bf16[1024,2048]{1,0:T(8,128)(2,1)} %fusion.106, bf16[1024,2048]{1,0:T(8,128)(2,1)} %copy-done.33), kind=kOutput, calls=%fused_computation.126 | convolution fusion | flops 8589934592 | bytes 25165824 | tf_op jit(solution)/shard_map/dot_general | solution.py:218
  350.3 8.6 all-gather.4
  358.9 8.3 all-gather.3
  370.3 54.7 %all-reduce.14.cloned.1.call-done = bf16[1024,2048]{1,0:T(8,128)(2,1)} async-done(((bf16[1024,2048]{1,0:T(8,128)(2,1)}), bf16[1024,2048]{1,0:T(8,128)(2,1)}) %all-reduce.14.cloned.1.call-update) | async-done | bytes 4194320 | tf_op jit(solution)/shard_map/psum | solution.py:241
  431.2 285.9 %all-reduce.12.cloned.1.call-done = f32[1024,2048]{1,0:T(8,128)} async-done(((f32[1024,2048]{1,0:T(8,128)}), f32[1024,2048]{1,0:T(8,128)}) %all-reduce.12.cloned.1.call-update) | async-done | bytes 8388624 | tf_op jit(solution)/shard_map/psum | solution.py:196
  717.2 13.4 %convert_reduce_fusion.2 = (f32[2048]{0:T(1024)S(1)}, f32[1024,2048]{1,0:T(8,128)}, bf16[1024,2048]{1,0:T(8,128)(2,1)}) fusion(bf16[1024,2048]{1,0:T(8,128)(2,1)} %param.31, f32[1024]{0:T(1024)S(1)} %broadcast_multiply_fusion.1, f32[1024]{0:T(1024)S(1)} %copy-done.22, bf16[1024,2048]{1,0:T(8,128)(2,1)} %param.18, f32[1024]{0:T(1024)S(1)} %broadcast_multiply_fusion.2, ...), kind=kLoop, calls=%fused_computation.89 | loop fusion | flops 33552384 | bytes 33603584 | tf_op jit(solution)/shard_map/reduce_sum | solution.py:206
  730.6 25.7 %all-reduce.8 = (f32[2048]{0:T(1024)S(1)}, f32[2048]{0:T(1024)S(1)}, f32[2,8,64]{2,1,0:T(8,128)S(1)}, f32[8,32]{0,1:T(8,128)S(1)}, f32[2048]{0:T(1024)S(1)}, /*index=5*/f32[32,64]{1,0:T(8,128)S(1)}) all-reduce(f32[2048]{0:T(1024)S(1)} %get-tuple-element.247, ...), channel_id=2, replica_groups=mesh['dp'=8,'tensor'=4] {'dp'}, use_global_device_ids=true, to_apply=%region_16.17.clone | all-reduce | flops 9472 | bytes 75776
  759.6 12.1 %reduce-scatter.9.cloned.1.call-done = f32[512,256]{1,0:T(8,128)} async-done(((f32[512,2048]{1,0:T(8,128)}), f32[512,256]{1,0:T(8,128)}) %reduce-scatter.9.cloned.1.call-update) | async-done | bytes 524304 | tf_op jit(solution)/shard_map/reduce_scatter | solution.py:260
  771.7 96.2 %reduce-scatter.7.cloned.1.call-done = f32[256,3,512]{2,0,1:T(8,128)} async-done(((f32[2048,3,512]{2,0,1:T(8,128)}), f32[256,3,512]{2,0,1:T(8,128)}) %reduce-scatter.7.cloned.1.call-update) | async-done | bytes 1572880 | tf_op jit(solution)/shard_map/reduce_scatter | solution.py:257
  867.9 120.1 %reduce-scatter.13.cloned.1.call-done = f32[2048,256]{1,0:T(8,128)} async-done(((f32[2048,2048]{1,0:T(8,128)}), f32[2048,256]{1,0:T(8,128)}) %reduce-scatter.13.cloned.1.call-update) | async-done | bytes 2097168 | tf_op jit(solution)/shard_map/reduce_scatter | solution.py:264
  988.0 120.2 %reduce-scatter.11.cloned.1.call-done = f32[256,2048]{1,0:T(8,128)} async-done(((f32[2048,2048]{1,0:T(8,128)}), f32[256,2048]{1,0:T(8,128)}) %reduce-scatter.11.cloned.1.call-update) | async-done | bytes 2097168 | tf_op jit(solution)/shard_map/reduce_scatter | solution.py:262
  (205 shorter events, 106.2 us)
Async XLA Ops:
  7.2 34.6 %copy-start.28 = (bf16[8,4]{0,1:T(4,128)(2,1)S(1)}, bf16[8,4]{0,1:T(4,128)(2,1)}, u32[]{:S(2)}) copy-start(bf16[8,4]{0,1:T(4,128)(2,1)} %param.24) | copy-start | bytes 196
  7.2 42.6 %copy-start.27 = (bf16[32,8]{0,1:T(8,128)(2,1)S(1)}, bf16[32,8]{0,1:T(8,128)(2,1)}, u32[]{:S(2)}) copy-start(bf16[32,8]{0,1:T(8,128)(2,1)} %param.28) | copy-start | bytes 1540
  7.2 67.5 %all-gather.12.cloned.1.call-start = ((), (), s32[]{:S(2)}) async-start(), calls=%async_computation.5 | async-start | bytes 2359296 | tf_op jit(solution)/shard_map/all_gather | solution.py:123
  7.9 81.4 %all-gather.10.cloned.1.call-start = ((), (), s32[]{:S(2)}) async-start(), calls=%async_computation.4 | async-start | bytes 7077888 | tf_op jit(solution)/shard_map/all_gather | solution.py:120
  10.3 201.2 %all-gather.14.cloned.1.call-start = ((), (), s32[]{:S(2)}) async-start(), calls=%async_computation.6 | async-start | bytes 9437184 | tf_op jit(solution)/shard_map/all_gather | solution.py:125
  11.0 216.1 %all-gather.16.cloned.1.call-start = ((), (), s32[]{:S(2)}) async-start(), calls=%async_computation.7 | async-start | bytes 9437184 | tf_op jit(solution)/shard_map/all_gather | solution.py:127
  11.6 413.4 %all-reduce.14.cloned.1.call-start = ((), (), s32[]{:S(2)}) async-start(), calls=%async_computation.9 | async-start | bytes 8388608 | tf_op jit(solution)/shard_map/psum | solution.py:241
  18.7 62.2 %copy-start.21 = (f32[1024]{0:T(1024)}, f32[1024]{0:T(1024)S(1)}, u32[]{:S(2)}) copy-start(f32[1024]{0:T(1024)S(1)} %broadcast_multiply_fusion.3) | copy-start | bytes 12292
  22.2 58.6 %copy-start.23 = (f32[1024]{0:T(1024)}, f32[1024]{0:T(1024)S(1)}, u32[]{:S(2)}) copy-start(f32[1024]{0:T(1024)S(1)} %add_rsqrt_fusion) | copy-start | bytes 12292
  41.7 39.1 %copy-start.19 = (f32[8,1,256]{2,1,0:T(1,128)}, f32[8,1,256]{2,1,0:T(1,128)S(1)}, u32[]{:S(2)}) copy-start(f32[8,1,256]{2,1,0:T(1,128)S(1)} %convert_element_type.142) | copy-start | bytes 24580
  115.0 88.3 %copy-start.18 = (f32[2,512,16]{1,2,0:T(8,128)S(1)}, f32[2,512,16]{1,2,0:T(8,128)}, u32[]{:S(2)}) copy-start(f32[2,512,16]{1,2,0:T(8,128)} %get-tuple-element.316) | copy-start | bytes 196612
  115.0 5.1 copy-start.1
  115.0 5.1 copy-start.6
  115.1 8.7 copy-start.3
  157.5 8.2 copy-start.3
  200.6 6.3 copy-start.8
  211.5 45.9 %copy-start.14 = (bf16[192,8,2,512]{3,1,2,0:T(8,128)(2,1)}, bf16[192,8,2,512]{3,1,2,0:T(8,128)(2,1)S(1)}, u32[]{:S(2)}) copy-start(bf16[192,8,2,512]{3,1,2,0:T(8,128)(2,1)S(1)} %copy.149) | copy-start | bytes 9437188
  211.5 15.6 %copy-start.25 = (f32[2048]{0:T(1024)S(1)}, f32[2048]{0:T(1024)}, u32[]{:S(2)}) copy-start(f32[2048]{0:T(1024)} %reshape.385) | copy-start | bytes 24580
  227.1 19.2 %copy-start.29 = (bf16[2048,2048]{1,0:T(8,128)(2,1)S(1)}, bf16[2048,2048]{1,0:T(8,128)(2,1)}, u32[]{:S(2)}) copy-start(bf16[2048,2048]{1,0:T(8,128)(2,1)} %all-gather.14.cloned.1.call-done) | copy-start | bytes 25165828
  246.3 11.1 copy-start.33
  270.1 447.1 %all-reduce.12.cloned.1.call-start = ((), (), s32[]{:S(2)}) async-start(), calls=%async_computation.8 | async-start | bytes 16777216 | tf_op jit(solution)/shard_map/psum | solution.py:196
  272.7 16.4 %copy-start.15 = (bf16[512,2048]{1,0:T(8,128)(2,1)S(1)}, bf16[512,2048]{1,0:T(8,128)(2,1)}, u32[]{:S(2)}) copy-start(bf16[512,2048]{1,0:T(8,128)(2,1)} %all-gather.12.cloned.1.call-done) | copy-start | bytes 6291460
  294.8 476.9 %reduce-scatter.9.cloned.1.call-start = ((), (), s32[]{:S(2)}) async-start(), calls=%async_computation.11 | async-start | bytes 4718592 | tf_op jit(solution)/shard_map/reduce_scatter | solution.py:260
  301.5 566.4 %reduce-scatter.7.cloned.1.call-start = ((), (), s32[]{:S(2)}) async-start(), calls=%async_computation.10 | async-start | bytes 14155776 | tf_op jit(solution)/shard_map/reduce_scatter | solution.py:257
  314.2 673.8 %reduce-scatter.13.cloned.1.call-start = ((), (), s32[]{:S(2)}) async-start(), calls=%async_computation.13 | async-start | bytes 18874368 | tf_op jit(solution)/shard_map/reduce_scatter | solution.py:264
  331.6 776.7 %reduce-scatter.11.cloned.1.call-start = ((), (), s32[]{:S(2)}) async-start(), calls=%async_computation.12 | async-start | bytes 18874368 | tf_op jit(solution)/shard_map/reduce_scatter | solution.py:262
  347.1 20.1 %copy-start.9 = (f32[2,1,512,8,64]{2,4,3,1,0:T(8,128)S(1)}, f32[2,1,512,8,64]{2,4,3,1,0:T(8,128)}, u32[]{:S(2)}) copy-start(f32[2,1,512,8,64]{2,4,3,1,0:T(8,128)} %get-tuple-element.109) | copy-start | bytes 6291460
  347.1 21.7 %copy-start.5 = (f32[2,512,8,32]{1,3,2,0:T(8,128)S(1)}, f32[2,512,8,32]{1,3,2,0:T(8,128)}, u32[]{:S(2)}) copy-start(f32[2,512,8,32]{1,3,2,0:T(8,128)} %copy-done.4) | copy-start | bytes 3145732
  347.1 77.9 %copy-start.20 = (f32[8,1,256]{2,1,0:T(1,128)S(1)}, f32[8,1,256]{2,1,0:T(1,128)}, u32[]{:S(2)}) copy-start(f32[8,1,256]{2,1,0:T(1,128)} %copy-done.19) | copy-start | bytes 24580
  347.1 77.9 %copy-start.22 = (f32[1024]{0:T(1024)S(1)}, f32[1024]{0:T(1024)}, u32[]{:S(2)}) copy-start(f32[1024]{0:T(1024)} %copy-done.21) | copy-start | bytes 12292
  347.1 77.9 %copy-start.24 = (f32[1024]{0:T(1024)S(1)}, f32[1024]{0:T(1024)}, u32[]{:S(2)}) copy-start(f32[1024]{0:T(1024)} %copy-done.23) | copy-start | bytes 12292
  757.0 351.8 %copy-start.26 = (f32[256]{0:T(256)}, f32[256]{0:T(256)S(1)}, u32[]{:S(2)}) copy-start(f32[256]{0:T(256)S(1)} %dynamic-slice.9) | copy-start | bytes 3076
  (20 other events, 47.7 us)
Sparse Core Ops, SparseCore 0:
  9.9 30.8 all-gather.11
  42.6 46.6 all-gather.9
  91.2 54.2 all-gather.13
  147.2 55.8 all-gather.15
  270.2 154.7 all-reduce.13
  427.3 289.7 all-reduce.11
  721.1 50.5 reduce-scatter.8
  775.7 92.0 reduce-scatter.6
  872.0 115.9 reduce-scatter.12
  992.0 116.2 reduce-scatter.10
where the time goes:
time: 1120 us
  waiting for transfers between devices  695 us (62%)
  matrix products  232 us (21%)
  blocking collectives  87.8 us (8%)
  other arithmetic  44.5 us (4%)
  local copies, waits for them, and re-layouts  39 us (3%)
  between operations  17.1 us (2%)
    psum x1, waiting for transfers between devices, local(): summed_out = lax.psum(branches, 'tensor')  286 us
    reduce_scatter x1, waiting for transfers between devices, local(): lax.psum_scatter(grad_up, 'dp', scatter_dimension=0, tiled=True)  120 us
    reduce_scatter x1, waiting for transfers between devices, local(): lax.psum_scatter(grad_down, 'dp', scatter_dimension=1, tiled=True)  120 us
    reduce_scatter x1, waiting for transfers between devices, local(): lax.psum_scatter(grad_qkv, 'dp', scatter_dimension=0, tiled=True)  96.2 us
    psum x1, waiting for transfers between devices, local(): lax.psum(grad_normed_part.astype(jnp.bfloat16), 'tensor')  54.7 us
    dot_general x2, matrix products, attend_back_group(): jnp.einsum('nhqk,nqhd->nkhd', grad_scores, queries, preferred_element_typ...  30.2 us
    dot_general x2, matrix products, attend_back_group(): jnp.einsum('nhqk,nkhd->nqhd', grad_scores, key_rows, preferred_element_ty...  28.8 us
    unnamed x1, blocking collectives  25.7 us
  transfers between devices with their start and end apart: 10, of which 7 were waited for; matrix products, arithmetic and copies ran while one was open for 23% of the time, Pallas kernels for 0%

commit v1 on v0

--- a/solution.py
+++ b/solution.py
@@ -193,7 +193,7 @@
     )
     dense_shift = dense_shift_all.astype(jnp.float32)
     down_shift = down_shift_all.astype(jnp.float32)
-    summed_out = lax.psum(branches, "tensor")
+    summed_out = jnp.sum(lax.all_gather(branches, "tensor"), axis=0)
     block_output = (widened + summed_out + dense_shift + down_shift).astype(jnp.bfloat16)
     gain_back, qkv_back, dense_back, up_back, down_back = (
         lax.all_gather(norm_gain, "dp", axis=0, tiled=True),

time: 1120 us -> 1390 us (1.24)
  waiting for transfers between devices: 695 us -> 947 us
  other arithmetic: 44.5 us -> 61.5 us
    all_gather x0 -> x1, waiting for transfers between devices: none -> 556 us  [local(): summed_out = jnp.sum(lax.all_gather(branches, 'tensor'), axis=0)]
    psum x1 -> x0, waiting for transfers between devices: 286 us -> none  [local(): summed_out = lax.psum(branches, 'tensor')]
    reduce_sum x0 -> x1, other arithmetic: none -> 17.1 us  [local(): summed_out = jnp.sum(lax.all_gather(branches, 'tensor'), axis=0)]
  transfers between devices with their start and end apart: 10 -> 10, of which waited for: 7 -> 6; matrix products, arithmetic and copies ran while one was open for 23% -> 20% of each run, Pallas kernels for 0% -> 0%
where the time goes in v1:
time: 1390 us; the launch traced here: 1380 us
  waiting for transfers between devices  947 us (68%)
  matrix products  231 us (17%)
  blocking collectives  87 us (6%)
  other arithmetic  61.5 us (4%)
  local copies, waits for them, and re-layouts  39 us (3%)
  between operations  16.9 us (1%)
    all_gather x1, waiting for transfers between devices, local(): summed_out = jnp.sum(lax.all_gather(branches, 'tensor'), axis=0)  556 us
    reduce_scatter x1, waiting for transfers between devices, local(): lax.psum_scatter(grad_up, 'dp', scatter_dimension=0, tiled=True)  120 us
    reduce_scatter x1, waiting for transfers between devices, local(): lax.psum_scatter(grad_down, 'dp', scatter_dimension=1, tiled=True)  120 us
    reduce_scatter x1, waiting for transfers between devices, local(): lax.psum_scatter(grad_qkv, 'dp', scatter_dimension=0, tiled=True)  91.1 us
    psum x1, waiting for transfers between devices, local(): lax.psum(grad_normed_part.astype(jnp.bfloat16), 'tensor')  54.4 us
    dot_general x2, matrix products, attend_back_group(): jnp.einsum('nhqk,nqhd->nkhd', grad_scores, queries, preferred_element_typ...  30.2 us
    dot_general x2, matrix products, attend_back_group(): jnp.einsum('nhqk,nkhd->nqhd', grad_scores, key_rows, preferred_element_ty...  28.8 us
  transfers between devices with their start and end apart: 10, of which 6 were waited for; matrix products, arithmetic and copies ran while one was open for 20% of the time, Pallas kernels for 0%

profile of v1, /device:TPU:0, one launch (start us, length us, event | category | flops | bytes accessed | tf_op | source)
XLA Modules:
  0.0 1384.7 jit_solution(2574425530127385075)
XLA Ops:
  22.3 10.4 all-gather.2
  32.7 9.1 all-gather.1
  41.8 8.0 all-gather.3
  49.8 9.2 all_gather.51
  59.8 8.3 all_gather.47
  89.3 10.1 fusion.146
  101.6 13.5 while.26
  115.1 85.7 %while.27 = (s32[]{:T(128)}, f32[2,1,512,8,64]{2,4,3,1,0:T(8,128)}, f32[2,1,512,8,64]{2,4,3,1,0:T(8,128)}, f32[2,1,512,8,64]{2,4,3,1,0:T(8,128)}, bf16[2,1,512,8...) while((s32[]{:T(128)}, f32[2,1,512,8,64]{2,4,3,1,0:T(8,128)}, ...), condition=%wide.region_11.12_spmd, body=%wide.region_9.11_spmd.sunk | while | flops 1396712448 | bytes 159765776 | solution.py:220
  128.5 14.5 %fusion.204 = f32[2,1,512,8,64]{2,4,3,1,0:T(8,128)} fusion(f32[2,1,512,8,64]{2,4,3,1,0:T(8,128)} %get-tuple-element.472, s32[]{:T(128)S(6)} %copy.169, f32[8,512,512]{1,2,0:T(8,128)} %fusion.201, f32[8,512,512]{1,2,0:T(8,128)} %copy-done, f32[8,512]{1,0:T(8,128)S(1)} %dynamic-slice_bitcast_fusion.7, ...), kind=kOutput, calls=%fused_computation.46.clone.1 | convolution fusion | flops 291508736 | bytes 35685376 | tf_op jit(solution)/shard_map/while/body/eval_jaxpr/nhqk,nqhd->nkhd/dot_general | solution.py:95
  143.1 14.4 %fusion.203 = f32[2,1,512,8,64]{2,4,3,1,0:T(8,128)} fusion(f32[2,1,512,8,64]{2,4,3,1,0:T(8,128)} %get-tuple-element.471, s32[]{:T(128)S(6)} %copy.169, f32[8,512,512]{1,2,0:T(8,128)} %fusion.201, f32[8,512,512]{1,2,0:T(8,128)} %copy-done, f32[8,512]{1,0:T(8,128)S(1)} %dynamic-slice_bitcast_fusion.7, ...), kind=kOutput, calls=%fused_computation.44.clone.1 | convolution fusion | flops 291508736 | bytes 35685376 | tf_op jit(solution)/shard_map/while/body/eval_jaxpr/nhqk,nkhd->nqhd/dot_general | solution.py:92
  170.4 15.7 %fusion.204 = f32[2,1,512,8,64]{2,4,3,1,0:T(8,128)} fusion(f32[2,1,512,8,64]{2,4,3,1,0:T(8,128)} %get-tuple-element.472, s32[]{:T(128)S(6)} %copy.169, f32[8,512,512]{1,2,0:T(8,128)} %fusion.201, f32[8,512,512]{1,2,0:T(8,128)} %copy-done, f32[8,512]{1,0:T(8,128)S(1)} %dynamic-slice_bitcast_fusion.7, ...), kind=kOutput, calls=%fused_computation.46.clone.1 | convolution fusion | flops 291508736 | bytes 35685376 | tf_op jit(solution)/shard_map/while/body/eval_jaxpr/nhqk,nqhd->nkhd/dot_general | solution.py:95
  186.1 14.4 %fusion.203 = f32[2,1,512,8,64]{2,4,3,1,0:T(8,128)} fusion(f32[2,1,512,8,64]{2,4,3,1,0:T(8,128)} %get-tuple-element.471, s32[]{:T(128)S(6)} %copy.169, f32[8,512,512]{1,2,0:T(8,128)} %fusion.201, f32[8,512,512]{1,2,0:T(8,128)} %copy-done, f32[8,512]{1,0:T(8,128)S(1)} %dynamic-slice_bitcast_fusion.7, ...), kind=kOutput, calls=%fused_computation.44.clone.1 | convolution fusion | flops 291508736 | bytes 35685376 | tf_op jit(solution)/shard_map/while/body/eval_jaxpr/nhqk,nkhd->nqhd/dot_general | solution.py:92
  211.8 15.6 %fusion.147 = f32[1024,2048]{1,0:T(8,128)} fusion(bf16[1024,2048]{1,0:T(8,128)(2,1)} %fusion.106, bf16[2048,2048]{1,0:T(8,128)(2,1)} %all-gather.16.cloned.1.call-done), kind=kOutput, calls=%fused_computation.179 | convolution fusion | flops 8589934592 | bytes 20971520 | tf_op jit(solution)/shard_map/dot_general | solution.py:187
  227.3 18.9 %fusion.143 = (f32[2048]{0:T(1024)S(1)}, bf16[1024,2048]{1,0:T(8,128)(2,1)S(1)}) fusion(f32[1024,2048]{1,0:T(8,128)} %fusion.147, f32[2048]{0:T(1024)S(1)} %copy-done.25, bf16[1024,2048]{1,0:T(8,128)(2,1)} %param.31, bf16[2048,2048]{1,0:T(8,128)(2,1)} %all-gather.18.cloned.1.call-done), kind=kOutput, calls=%fused_computation.176 | convolution fusion | flops 8636069888 | bytes 25182208 | tf_op jit(solution)/shard_map/dot_general | solution.py:214
  246.3 11.1 fusion.129
  257.4 12.7 add_convert_fusion
  272.7 16.4 %fusion.142 = f32[1024,2048]{1,0:T(8,128)S(1)} fusion(bf16[2048,2048]{1,0:T(8,128)(2,1)} %all-gather.18.cloned.1.call-done, f32[1024,2048]{1,0:T(8,128)} %fusion.147, f32[2048]{0:T(1024)S(1)} %copy-done.25), kind=kOutput, calls=%fused_computation.175 | convolution fusion | flops 8610906112 | bytes 25174016 | tf_op jit(solution)/shard_map/dot_general | solution.py:191
  295.2 6.5 fusion.148
  301.8 12.6 fusion.121
  314.6 17.2 %fusion.141 = f32[2048,2048]{1,0:T(8,128)} fusion(bf16[1024,2048]{1,0:T(8,128)(2,1)} %param.31, f32[1024,2048]{1,0:T(8,128)} %fusion.147, f32[2048]{0:T(1024)S(1)} %copy-done.25), kind=kOutput, calls=%fused_computation.174 | convolution fusion | flops 8610906112 | bytes 29368320 | tf_op jit(solution)/shard_map/dot_general | solution.py:208
  332.1 15.2 %fusion.127 = f32[2048,2048]{1,0:T(8,128)} fusion(bf16[1024,2048]{1,0:T(8,128)(2,1)} %fusion.106, bf16[1024,2048]{1,0:T(8,128)(2,1)} %copy-done.33), kind=kOutput, calls=%fused_computation.126 | convolution fusion | flops 8589934592 | bytes 25165824 | tf_op jit(solution)/shard_map/dot_general | solution.py:218
  350.5 8.5 all-gather.5
  359.0 8.4 all-gather.4
  370.5 54.4 %all-reduce.11.cloned.1.call-done = bf16[1024,2048]{1,0:T(8,128)(2,1)} async-done(((bf16[1024,2048]{1,0:T(8,128)(2,1)}), bf16[1024,2048]{1,0:T(8,128)(2,1)}) %all-reduce.11.cloned.1.call-update) | async-done | bytes 4194320 | tf_op jit(solution)/shard_map/psum | solution.py:241
  424.8 6.2 fusion.120
  431.1 555.6 %all-gather.20.cloned.1.call-done = f32[4096,2048]{1,0:T(8,128)} async-done(((f32[1024,2048]{1,0:T(8,128)}), f32[4096,2048]{1,0:T(8,128)}) %all-gather.20.cloned.1.call-update) | async-done | bytes 33554448 | tf_op jit(solution)/shard_map/all_gather | solution.py:196
  986.6 17.1 %reduce_sum.128 = f32[1024,2048]{1,0:T(8,128)} reduce(f32[4,1024,2048]{2,1,0:T(8,128)} %bitcast.229, f32[]{:T(128)} %constant.72.clone.1), dimensions={0}, to_apply=%region_8.9 | reduce | flops 6291456 | bytes 41943044 | tf_op jit(solution)/shard_map/reduce_sum | solution.py:196
  1003.7 13.3 convert_reduce_fusion.2
  1017.0 25.3 %all-reduce.8 = (f32[2048]{0:T(1024)S(1)}, f32[2048]{0:T(1024)S(1)}, f32[2,8,64]{2,1,0:T(8,128)S(1)}, f32[8,32]{0,1:T(8,128)S(1)}, f32[2048]{0:T(1024)S(1)}, /*index=5*/f32[32,64]{1,0:T(8,128)S(1)}) all-reduce(f32[2048]{0:T(1024)S(1)} %get-tuple-element.247, ...), channel_id=3, replica_groups=mesh['dp'=8,'tensor'=4] {'dp'}, use_global_device_ids=true, to_apply=%region_16.17.clone | all-reduce | flops 9472 | bytes 75776
  1045.6 91.1 %reduce-scatter.7.cloned.1.call-done = f32[256,3,512]{2,0,1:T(8,128)} async-done(((f32[2048,3,512]{2,0,1:T(8,128)}), f32[256,3,512]{2,0,1:T(8,128)}) %reduce-scatter.7.cloned.1.call-update) | async-done | bytes 1572880 | tf_op jit(solution)/shard_map/reduce_scatter | solution.py:257
  1136.7 120.2 %reduce-scatter.13.cloned.1.call-done = f32[2048,256]{1,0:T(8,128)} async-done(((f32[2048,2048]{1,0:T(8,128)}), f32[2048,256]{1,0:T(8,128)}) %reduce-scatter.13.cloned.1.call-update) | async-done | bytes 2097168 | tf_op jit(solution)/shard_map/reduce_scatter | solution.py:264
  1256.9 120.2 %reduce-scatter.11.cloned.1.call-done = f32[256,2048]{1,0:T(8,128)} async-done(((f32[2048,2048]{1,0:T(8,128)}), f32[256,2048]{1,0:T(8,128)}) %reduce-scatter.11.cloned.1.call-update) | async-done | bytes 2097168 | tf_op jit(solution)/shard_map/reduce_scatter | solution.py:262
  (206 shorter events, 106.7 us)
Async XLA Ops:
  7.2 34.6 %copy-start.28 = (bf16[8,4]{0,1:T(4,128)(2,1)S(1)}, bf16[8,4]{0,1:T(4,128)(2,1)}, u32[]{:S(2)}) copy-start(bf16[8,4]{0,1:T(4,128)(2,1)} %param.24) | copy-start | bytes 196
  7.2 42.6 %copy-start.27 = (bf16[32,8]{0,1:T(8,128)(2,1)S(1)}, bf16[32,8]{0,1:T(8,128)(2,1)}, u32[]{:S(2)}) copy-start(bf16[32,8]{0,1:T(8,128)(2,1)} %param.28) | copy-start | bytes 1540
  7.2 67.2 %all-gather.14.cloned.1.call-start = ((), (), s32[]{:S(2)}) async-start(), calls=%async_computation.5 | async-start | bytes 2359296 | tf_op jit(solution)/shard_map/all_gather | solution.py:123
  7.9 81.4 %all-gather.12.cloned.1.call-start = ((), (), s32[]{:S(2)}) async-start(), calls=%async_computation.4 | async-start | bytes 7077888 | tf_op jit(solution)/shard_map/all_gather | solution.py:120
  10.3 201.5 %all-gather.16.cloned.1.call-start = ((), (), s32[]{:S(2)}) async-start(), calls=%async_computation.6 | async-start | bytes 9437184 | tf_op jit(solution)/shard_map/all_gather | solution.py:125
  11.0 216.3 %all-gather.18.cloned.1.call-start = ((), (), s32[]{:S(2)}) async-start(), calls=%async_computation.7 | async-start | bytes 9437184 | tf_op jit(solution)/shard_map/all_gather | solution.py:127
  11.6 413.2 %all-reduce.11.cloned.1.call-start = ((), (), s32[]{:S(2)}) async-start(), calls=%async_computation.8 | async-start | bytes 8388608 | tf_op jit(solution)/shard_map/psum | solution.py:241
  18.7 61.9 %copy-start.21 = (f32[1024]{0:T(1024)}, f32[1024]{0:T(1024)S(1)}, u32[]{:S(2)}) copy-start(f32[1024]{0:T(1024)S(1)} %broadcast_multiply_fusion.3) | copy-start | bytes 12292
  22.3 58.3 %copy-start.23 = (f32[1024]{0:T(1024)}, f32[1024]{0:T(1024)S(1)}, u32[]{:S(2)}) copy-start(f32[1024]{0:T(1024)S(1)} %add_rsqrt_fusion) | copy-start | bytes 12292
  41.8 38.8 %copy-start.19 = (f32[8,1,256]{2,1,0:T(1,128)}, f32[8,1,256]{2,1,0:T(1,128)S(1)}, u32[]{:S(2)}) copy-start(f32[8,1,256]{2,1,0:T(1,128)S(1)} %convert_element_type.142) | copy-start | bytes 24580
  115.1 88.5 %copy-start.18 = (f32[2,512,16]{1,2,0:T(8,128)S(1)}, f32[2,512,16]{1,2,0:T(8,128)}, u32[]{:S(2)}) copy-start(f32[2,512,16]{1,2,0:T(8,128)} %get-tuple-element.316) | copy-start | bytes 196612
  115.1 5.2 copy-start.1
  115.1 5.2 copy-start.6
  115.1 8.7 copy-start.3
  157.5 8.1 copy-start.3
  200.8 6.3 copy-start.8
  211.7 45.6 %copy-start.14 = (bf16[192,8,2,512]{3,1,2,0:T(8,128)(2,1)}, bf16[192,8,2,512]{3,1,2,0:T(8,128)(2,1)S(1)}, u32[]{:S(2)}) copy-start(bf16[192,8,2,512]{3,1,2,0:T(8,128)(2,1)S(1)} %copy.149) | copy-start | bytes 9437188
  211.7 15.6 %copy-start.25 = (f32[2048]{0:T(1024)S(1)}, f32[2048]{0:T(1024)}, u32[]{:S(2)}) copy-start(f32[2048]{0:T(1024)} %reshape.385) | copy-start | bytes 24580
  227.3 19.0 %copy-start.29 = (bf16[2048,2048]{1,0:T(8,128)(2,1)S(1)}, bf16[2048,2048]{1,0:T(8,128)(2,1)}, u32[]{:S(2)}) copy-start(bf16[2048,2048]{1,0:T(8,128)(2,1)} %all-gather.16.cloned.1.call-done) | copy-start | bytes 25165828
  246.3 11.1 copy-start.33
  270.1 716.6 %all-gather.20.cloned.1.call-start = ((), (), s32[]{:S(2)}) async-start(), calls=%async_computation.13 | async-start | bytes 41943040 | tf_op jit(solution)/shard_map/all_gather | solution.py:196
  272.7 16.4 %copy-start.15 = (bf16[512,2048]{1,0:T(8,128)(2,1)S(1)}, bf16[512,2048]{1,0:T(8,128)(2,1)}, u32[]{:S(2)}) copy-start(bf16[512,2048]{1,0:T(8,128)(2,1)} %all-gather.14.cloned.1.call-done) | copy-start | bytes 6291460
  294.8 750.8 %reduce-scatter.9.cloned.1.call-start = ((), (), s32[]{:S(2)}) async-start(), calls=%async_computation.10 | async-start | bytes 4718592 | tf_op jit(solution)/shard_map/reduce_scatter | solution.py:260
  301.8 834.9 %reduce-scatter.7.cloned.1.call-start = ((), (), s32[]{:S(2)}) async-start(), calls=%async_computation.9 | async-start | bytes 14155776 | tf_op jit(solution)/shard_map/reduce_scatter | solution.py:257
  314.5 942.4 %reduce-scatter.13.cloned.1.call-start = ((), (), s32[]{:S(2)}) async-start(), calls=%async_computation.12 | async-start | bytes 18874368 | tf_op jit(solution)/shard_map/reduce_scatter | solution.py:264
  331.8 1045.3 %reduce-scatter.11.cloned.1.call-start = ((), (), s32[]{:S(2)}) async-start(), calls=%async_computation.11 | async-start | bytes 18874368 | tf_op jit(solution)/shard_map/reduce_scatter | solution.py:262
  347.3 20.1 %copy-start.9 = (f32[2,1,512,8,64]{2,4,3,1,0:T(8,128)S(1)}, f32[2,1,512,8,64]{2,4,3,1,0:T(8,128)}, u32[]{:S(2)}) copy-start(f32[2,1,512,8,64]{2,4,3,1,0:T(8,128)} %get-tuple-element.109) | copy-start | bytes 6291460
  347.3 21.7 %copy-start.5 = (f32[2,512,8,32]{1,3,2,0:T(8,128)S(1)}, f32[2,512,8,32]{1,3,2,0:T(8,128)}, u32[]{:S(2)}) copy-start(f32[2,512,8,32]{1,3,2,0:T(8,128)} %copy-done.4) | copy-start | bytes 3145732
  347.3 77.5 %copy-start.20 = (f32[8,1,256]{2,1,0:T(1,128)S(1)}, f32[8,1,256]{2,1,0:T(1,128)}, u32[]{:S(2)}) copy-start(f32[8,1,256]{2,1,0:T(1,128)} %copy-done.19) | copy-start | bytes 24580
  347.3 77.5 %copy-start.22 = (f32[1024]{0:T(1024)S(1)}, f32[1024]{0:T(1024)}, u32[]{:S(2)}) copy-start(f32[1024]{0:T(1024)} %copy-done.21) | copy-start | bytes 12292
  347.3 77.5 %copy-start.24 = (f32[1024]{0:T(1024)S(1)}, f32[1024]{0:T(1024)}, u32[]{:S(2)}) copy-start(f32[1024]{0:T(1024)} %copy-done.23) | copy-start | bytes 12292
  1043.0 334.7 %copy-start.26 = (f32[256]{0:T(256)}, f32[256]{0:T(256)S(1)}, u32[]{:S(2)}) copy-start(f32[256]{0:T(256)S(1)} %dynamic-slice.9) | copy-start | bytes 3076
  (20 other events, 47.7 us)
Sparse Core Ops, SparseCore 0:
  9.9 30.8 all-gather.13
  42.6 46.6 all-gather.11
  91.2 54.2 all-gather.15
  147.2 55.8 all-gather.17
  270.2 154.5 all-reduce.10
  426.3 560.3 all-gather.19
  990.6 50.0 reduce-scatter.8
  1044.7 91.9 reduce-scatter.6
  1140.9 115.9 reduce-scatter.12
  1260.9 116.1 reduce-scatter.10
